TPU v7x, 512 devices: a 8x2x16 block of a 8x8x16 slice. The times are simulated.
512 devices in a mesh: groups: 2 (over y), wide: 128 (over x, z), narrow: 2 (over core).
Axes of the slice: x: 8, y: 2, z: 16, core: 2. Of those that a mesh axis runs over, the one named last changes fastest.
The devices are a block of a 8x8x16 slice.
Arguments:
- hidden_in: bfloat16 [102400, 1024], P(('groups', 'wide')), parts along dimension 0, may hold values from -6 to 6
- ffn_gain: bfloat16 [1024], replicated, may hold values from 0.5 to 1.5
- wi_gate: bfloat16 [1024, 2816], P('wide', 'narrow'), may hold values from -0.1875 to 0.1875
- wi_up: bfloat16 [1024, 2816], P('wide', 'narrow'), may hold values from -0.1875 to 0.1875
- wo_down: bfloat16 [2816, 1024], P('narrow', 'wide'), may hold values from -0.109375 to 0.109375
- final_gain: bfloat16 [1024], replicated, may hold values from 0.5 to 1.5
- key_w: bfloat16 [1024, 1024], P('wide', 'narrow'), may hold values from -0.1875 to 0.1875
- value_w: bfloat16 [1024, 1024], P('wide', 'narrow'), may hold values from -0.1875 to 0.1875
- query_w: bfloat16 [1024, 1024], P('wide', 'narrow'), may hold values from -8 to 8
- out_w: bfloat16 [1024, 1024], P('narrow', 'wide'), may hold values from -0.1875 to 0.1875
- dec_gain: bfloat16 [1024], replicated, may hold values from 0.5 to 1.5
- embed: bfloat16 [32128, 1024], P('wide'), may hold values from -6 to 6
- lengths: int32 [512], P(('groups', 'wide')), parts along dimension 0, may hold values from 40 to 200
- answer_ids: int32 [8, 32], P('groups'), parts along dimension 0, may hold values from 0 to 32127
Outputs:
- memory: bfloat16 [102400, 1024], P(('groups', 'wide')), parts along dimension 0
- decoded: bfloat16 [256, 1024], P('groups', 'narrow'), parts along dimension 0
There are 2 independent parts, one for each index of `groups`. A program takes and returns all parts, laid end to end along the dimension named above; an argument that names none is the same for every part. Nothing has to cross between parts.
All inputs are finite; a program needn't handle non-finite values.
Results may differ from a plain program's by a relative error of at most 0.0095.
The roundings to bfloat16 on the way count: a program that leaves them out, or rounds other values in their place, can miss the bound.
Values may be sent and summed in bfloat16 or wider, within the bound.
A program may use at most 64 MiB of HBM per device.

v0:
```python
import math
import jax
import jax.numpy as jnp
from jax import lax
from jax.sharding import Mesh
from jax.sharding import PartitionSpec as P

HEAD_DIM = 64
QUEST = 4
WIDE = ("wide_0", "wide_1")
GROUPS_WIDE = ("groups", "wide_0", "wide_1")
EPS = 1e-06
FLOOR = -1e30


def in_one_piece(arrays, axis, dim, along):
    ends, at = ([], 0)
    for a in arrays[:-1]:
        at += a.shape[along]
        ends.append(at)
    both = jnp.concatenate(arrays, axis=along)
    return tuple(jnp.split(lax.all_gather(both, axis, axis=dim, tiled=True), ends, axis=along))


def in_order(tiles, dim):
    tiles = jnp.moveaxis(tiles, 0, dim)
    lengths = tiles.shape
    return tiles.reshape(*lengths[:dim], lengths[dim] * lengths[dim + 1], *lengths[dim + 2 :])


def all_blocks(x, axes, turns):
    tiles = x
    for k in turns:
        tiles = lax.all_gather(tiles, axes[k])
    done = turns[::-1]
    back = [done.index(k) for k in range(len(axes))]
    tiles = tiles.transpose(*back, *range(len(axes), tiles.ndim))
    return tiles.reshape(-1, *x.shape)


def whole_of(x, axes, turns, dim):
    return in_order(all_blocks(x, axes, turns), dim)


def from_everyone(x, axis):
    copies = jnp.broadcast_to(x, (lax.axis_size(axis), *x.shape))
    return lax.all_to_all(copies, axis, split_axis=0, concat_axis=0, tiled=True)


def over_copies(x, axis):
    return from_everyone(x, axis).sum(axis=0)


def collected_together(x, axis):
    leaves = jax.tree.leaves(x)
    turns = sorted(range(len(leaves)), key=lambda k: -leaves[k].size)
    width = (1, *leaves[turns[0]].shape)[-1]
    lines = [
        jnp.pad(leaves[k].reshape(-1), (0, -leaves[k].size % width)).reshape(-1, width)
        for k in turns
    ]
    both, at, found = (lax.all_gather(jnp.concatenate(lines), axis), 0, {})
    for k, line in zip(turns, lines):
        piece = both[:, at : at + len(line)].reshape(len(both), -1)
        found[k] = piece[:, : leaves[k].size].reshape(-1, *leaves[k].shape)
        at += len(line)
    numbers = iter(range(len(leaves)))
    return jax.tree.map(lambda _: found[next(numbers)], x)


def joined_all(x, axes, combine):
    for axis in axes:
        pieces = collected_together(x, axis)
        x = jax.tree.map(lambda part: part[0], pieces)
        for k in range(1, lax.axis_size(axis)):
            x = combine(x, jax.tree.map(lambda part: part[k], pieces))
    return x


def split_up(x, dim, devices):
    lengths = x.shape
    tiles = x.reshape(*lengths[:dim], devices, lengths[dim] // devices, *lengths[dim + 1 :])
    return jnp.moveaxis(tiles, dim, 0)


def sum_at_owner(x, axis, dim):
    tiles = split_up(x, dim, lax.axis_size(axis))
    arrived = lax.all_to_all(tiles, axis, split_axis=0, concat_axis=0, tiled=True)
    return arrived.astype(jnp.float32).sum(axis=0)


def rms_scale(values, gain):
    mean_square = jnp.mean(values * values, axis=-1, keepdims=True)
    return values * lax.rsqrt(mean_square + EPS) * gain.astype(jnp.float32)


def join_partial(first, second):
    top_first, total_first, acc_first = first
    top_second, total_second, acc_second = second
    top = jnp.maximum(top_first, top_second)
    factor_first = jnp.exp(top_first - top)
    factor_second = jnp.exp(top_second - top)
    width = acc_first.shape[1] // top.shape[1]
    total = total_first * factor_first + total_second * factor_second
    acc = acc_first * jnp.repeat(factor_first, width, axis=1) + acc_second * jnp.repeat(
        factor_second, width, axis=1
    )
    return (top, total, acc)


def per_device(
    hidden_in,
    ffn_gain,
    wi_gate,
    wi_up,
    wo_down,
    final_gain,
    key_w,
    value_w,
    query_w,
    out_w,
    dec_gain,
    embed,
    lengths,
    answer_ids,
):
    rows = hidden_in.shape[0]
    resid_in = hidden_in.astype(jnp.float32)
    enc_in = rms_scale(resid_in, ffn_gain).astype(jnp.bfloat16)
    gate_full, up_full = in_one_piece((wi_gate, wi_up), WIDE, 0, 1)
    gate = jnp.dot(enc_in, gate_full, preferred_element_type=jnp.float32)
    up = jnp.dot(enc_in, up_full, preferred_element_type=jnp.float32)
    inner = (jax.nn.gelu(gate, approximate=True) * up).astype(jnp.bfloat16)
    down_full = whole_of(wo_down, WIDE, (0, 1), 1)
    partial_down = jnp.dot(inner, down_full, preferred_element_type=jnp.float32)
    resid = resid_in + over_copies(partial_down, "narrow")
    memory = rms_scale(resid, final_gain).astype(jnp.bfloat16)
    pass_dev = lengths.shape[0]
    per_question = pass_dev * lax.axis_size(WIDE) // QUEST
    question = lax.axis_index(WIDE) * pass_dev // per_question
    answers = answer_ids.shape[1]
    qrows = answer_ids.shape[0] * answers
    vocab_rows = embed.shape[0]
    local_ids = answer_ids.reshape(qrows) - lax.axis_index(WIDE) * vocab_rows
    onehot = (local_ids[:, None] == jnp.arange(vocab_rows, dtype=jnp.int32)[None, :]).astype(
        jnp.bfloat16
    )
    embedded = lax.psum(jnp.dot(onehot, embed, preferred_element_type=jnp.float32), WIDE)
    dec_in = rms_scale(embedded, dec_gain).astype(jnp.bfloat16)
    own_rows = lax.dynamic_slice_in_dim(dec_in, question * answers, answers, 0)
    proj_cols = key_w.shape[1]
    key_full, value_full, query_full = in_one_piece((key_w, value_w, query_w), WIDE, 0, 1)
    keys_sum = jnp.dot(memory, key_full, preferred_element_type=jnp.float32)
    values_sum = jnp.dot(memory, value_full, preferred_element_type=jnp.float32)
    query_sum = jnp.dot(own_rows, query_full, preferred_element_type=jnp.float32)
    keys = keys_sum.astype(jnp.bfloat16)
    values = values_sum.astype(jnp.bfloat16)
    query = query_sum.astype(jnp.bfloat16)
    heads_local = proj_cols // HEAD_DIM
    query_three = query.reshape(answers, heads_local, HEAD_DIM)
    keys_three = keys.reshape(rows, heads_local, HEAD_DIM)
    values_three = values.reshape(rows, heads_local, HEAD_DIM).astype(jnp.float32)
    scores = jnp.einsum(
        "ahd,khd->ahk", query_three, keys_three, preferred_element_type=jnp.float32
    ) * (1.0 / math.sqrt(HEAD_DIM))
    passage_len = rows // pass_dev
    live = (jnp.arange(passage_len, dtype=jnp.int32)[None, :] < lengths[:, None]).reshape(rows)
    scores = jnp.where(live[None, None, :], scores, FLOOR)
    top = jnp.max(scores, axis=2)
    weights = jnp.exp(scores - top[:, :, None])
    total = jnp.sum(weights, axis=2)
    acc = jnp.einsum("ahk,khd->ahd", weights, values_three).reshape(answers, proj_cols)
    start_row = question * answers
    top_all = lax.dynamic_update_slice_in_dim(
        jnp.full((qrows, heads_local), FLOOR, jnp.float32), top, start_row, 0
    )
    total_all = lax.dynamic_update_slice_in_dim(
        jnp.zeros((qrows, heads_local), jnp.float32), total, start_row, 0
    )
    acc_all = lax.dynamic_update_slice_in_dim(
        jnp.zeros((qrows, proj_cols), jnp.float32), acc, start_row, 0
    )
    top_all, total_all, acc_all = joined_all((top_all, total_all, acc_all), WIDE, join_partial)
    attended = (acc_all / jnp.repeat(total_all, HEAD_DIM, axis=1)).astype(jnp.bfloat16)
    out_full = whole_of(out_w, WIDE, (0, 1), 1)
    partial_out = jnp.dot(attended, out_full, preferred_element_type=jnp.float32)
    share_out = sum_at_owner(partial_out.astype(jnp.bfloat16), "narrow", 1)
    out_half = share_out.shape[1]
    embedded_half = lax.dynamic_slice_in_dim(
        embedded, lax.axis_index("narrow") * out_half, out_half, 1
    )
    decoded = (embedded_half + share_out).astype(jnp.bfloat16)
    return (memory, decoded)


def solution(mesh):
    torus = Mesh(
        mesh.devices.reshape(mesh.shape["groups"], 8, 16, mesh.shape["narrow"]),
        ("groups", "wide_0", "wide_1", "narrow"),
    )
    return jax.shard_map(
        per_device,
        mesh=torus,
        in_specs=(
            P(GROUPS_WIDE, None),
            P(),
            P(WIDE, "narrow"),
            P(WIDE, "narrow"),
            P("narrow", WIDE),
            P(),
            P(WIDE, "narrow"),
            P(WIDE, "narrow"),
            P(WIDE, "narrow"),
            P("narrow", WIDE),
            P(),
            P(WIDE, None),
            P(GROUPS_WIDE),
            P("groups", None),
        ),
        out_specs=(P(GROUPS_WIDE, None), P("groups", "narrow")),
        check_vma=False,
    )
```

profile of v0, /device:TPU:65, one launch (start us, length us, event | category | flops | bytes accessed | tf_op | source)
XLA Modules:
  0.0 730.1 jit_solution(12528337579370721748)
XLA Ops:
  8.2 0.8 broadcast_subtract_fusion
  9.1 1.1 fusion.40
  10.3 23.2 %all-gather = bf16[11264,8]{0,1:T(8,128)(2,1)} all-gather(bf16[1408,8]{0,1:T(8,128)(2,1)} %param.18), channel_id=2, replica_groups=mesh['groups'=2,'wide_0'=8,'wide_1'=16,'narrow'=2] {'wide_0'}, dimensions={0}, use_global_device_ids=true | all-gather | bytes 202752 | tf_op jit(solution)/shard_map/all_gather | solution.py:34
  33.6 1.3 pad_maximum_fusion.1
  35.1 1.4 pad_maximum_fusion
  36.6 0.7 convert_element_type.57
  37.3 0.7 convert_element_type.60
  38.4 277.3 %all-reduce.2.cloned.1.call-done = f32[128,1024]{1,0:T(8,128)} async-done(((f32[128,1024]{1,0:T(8,128)}), f32[128,1024]{1,0:T(8,128)}) %all-reduce.2.cloned.1.call-update) | async-done | bytes 524304 | tf_op jit(solution)/shard_map/psum | solution.py:148
  315.7 1.2 multiply_reduce_fusion.1
  317.0 3.8 copy.413
  320.8 1.5 convolution_convert_fusion.3
  322.3 0.7 reshape.508
  323.1 111.4 %all-gather.15.cloned.1.call-done = bf16[1024,2816]{1,0:T(8,128)(2,1)} async-done(((bf16[8,2816]{1,0:T(8,128)(2,1)}), bf16[1024,2816]{1,0:T(8,128)(2,1)}) %all-gather.15.cloned.1.call-update) | async-done | bytes 5767184 | tf_op jit(solution)/shard_map/all_gather | solution.py:22
  434.4 4.9 fusion.12
  439.4 6.1 fusion.24
  445.9 15.5 %all_to_all.10 = f32[2,400,1024]{2,1,0:T(8,128)} all-to-all(f32[2,400,1024]{2,1,0:T(8,128)S(1)} %broadcast_in_dim.170), channel_id=1, replica_groups=mesh['groups'=2,'wide_0'=8,'wide_1'=16,'narrow'=2] {'narrow'}, dimensions={0} | all-to-all | bytes 6553600 | tf_op jit(solution)/shard_map/all_to_all | solution.py:47
  461.4 2.4 reduce_sum.55
  464.4 0.9 copy-done.3
  465.3 1.8 convolution_convert_fusion
  468.3 1.8 convolution_convert_fusion.1
  470.9 0.7 maximum_bitcast_fusion.1
  471.7 21.1 %all-gather.4 = bf16[4096,8]{0,1:T(8,128)(2,1)} all-gather(bf16[512,8]{0,1:T(8,128)(2,1)S(1)} %copy-done.8), channel_id=6, replica_groups=mesh['groups'=2,'wide_0'=8,'wide_1'=16,'narrow'=2] {'wide_0'}, dimensions={0}, use_global_device_ids=true | all-gather | bytes 73728 | tf_op jit(solution)/shard_map/all_gather | solution.py:34
  493.2 16.7 %all-gather.23.cloned.1.call-done = f32[8,132,512]{2,1,0:T(8,128)} async-done(((f32[1,132,512]{2,1,0:T(8,128)}), f32[8,132,512]{2,1,0:T(8,128)}) %all-gather.23.cloned.1.call-update) | async-done | bytes 2162704 | tf_op jit(solution)/shard_map/all_gather | solution.py:62
  509.8 1.0 fusion.51
  511.2 2.6 fusion.96
  514.4 1.1 copy.515
  515.5 1.8 copy.514
  517.3 0.8 copy.513
  518.1 0.8 fusion.95
  520.4 1.2 fusion.27
  521.7 0.9 copy.446
  522.7 54.6 %all-gather.21.cloned.1.call-done = bf16[128,512,8]{1,2,0:T(8,128)(2,1)} async-done(((bf16[8,512,8]{1,2,0:T(8,128)(2,1)}), bf16[128,512,8]{1,2,0:T(8,128)(2,1)}) %all-gather.21.cloned.1.call-update) | async-done | bytes 1048592 | tf_op jit(solution)/shard_map/all_gather | solution.py:34
  577.2 1.3 copy.511
  578.6 79.3 %all-gather.25.cloned.1.call-done = f32[16,132,512]{2,1,0:T(8,128)} async-done(((f32[1,132,512]{2,1,0:T(8,128)}), f32[16,132,512]{2,1,0:T(8,128)}) %all-gather.25.cloned.1.call-update) | async-done | bytes 4325392 | tf_op jit(solution)/shard_map/all_gather | solution.py:62
  657.8 3.8 fusion.94
  662.2 1.1 copy.532
  663.3 1.8 copy.531
  665.1 1.8 copy.530
  666.9 1.8 copy.529
  668.7 1.8 copy.528
  670.5 1.8 copy.527
  672.3 1.8 copy.526
  674.1 1.8 copy.525
  675.8 1.8 copy.524
  677.6 1.8 copy.523
  679.4 1.8 copy.522
  681.2 1.8 copy.521
  683.0 1.5 fusion.93
  685.5 1.6 fusion.92
  687.0 0.8 squeeze.305
  688.5 0.8 squeeze.304
  689.9 0.8 squeeze.303
  692.2 0.7 copy.500
  696.6 0.8 squeeze.265
  698.6 0.8 squeeze.276
  699.5 0.8 squeeze.274
  700.3 0.8 squeeze.272
  701.1 0.8 squeeze.270
  702.3 0.8 squeeze.292
  703.8 0.8 squeeze.294
  705.2 1.0 multiply_add_fusion
  706.2 2.6 divide_convert_fusion
  709.3 12.7 %all_to_all.11 = bf16[2,128,512]{2,1,0:T(8,128)(2,1)S(1)} all-to-all(bf16[2,128,512]{2,1,0:T(8,128)(2,1)S(1)} %bitcast.360), channel_id=1, replica_groups=mesh['groups'=2,'wide_0'=8,'wide_1'=16,'narrow'=2] {'narrow'}, dimensions={0} | all-to-all | bytes 524288 | tf_op jit(solution)/shard_map/all_to_all | solution.py:88
  722.0 0.7 add_convert_fusion
  (154 shorter events, 18.3 us)
Async XLA Ops:
  8.0 1.0 copy-start
  8.1 30.0 %copy-start.9 = (bf16[1024]{0:T(1024)(128)(2,1)S(1)}, bf16[1024]{0:T(1024)(128)(2,1)}, u32[]{:S(2)}) copy-start(bf16[1024]{0:T(1024)(128)(2,1)} %param.24) | copy-start | bytes 6148
  8.1 30.0 %copy-start.10 = (s32[2]{0:T(128)S(1)}, s32[2]{0:T(128)}, u32[]{:S(2)}) copy-start(s32[2]{0:T(128)} %param.26) | copy-start | bytes 28
  8.1 30.1 %copy-start.1 = (bf16[400,1024]{1,0:T(8,128)(2,1)S(1)}, bf16[400,1024]{1,0:T(8,128)(2,1)}, u32[]{:S(2)}) copy-start(bf16[400,1024]{1,0:T(8,128)(2,1)} %param.14) | copy-start | bytes 2457604
  8.1 307.7 %all-reduce.2.cloned.1.call-start = ((), (), s32[]{:S(2)}) async-start(), calls=%async_computation.3 | async-start | bytes 1048576 | tf_op jit(solution)/shard_map/psum | solution.py:148
  10.2 306.8 %all-gather.19.cloned.1.call-start = ((), (), s32[]{:S(2)}) async-start(), calls=%async_computation.5 | async-start | bytes 3063808 | tf_op jit(solution)/shard_map/all_gather | solution.py:34
  33.6 287.2 %all-gather.17.cloned.1.call-start = ((), (), s32[]{:S(2)}) async-start(), calls=%async_computation.4 | async-start | bytes 3170304 | tf_op jit(solution)/shard_map/all_gather | solution.py:22
  35.0 399.4 %all-gather.15.cloned.1.call-start = ((), (), s32[]{:S(2)}) async-start(), calls=%async_computation.2 | async-start | bytes 5812224 | tf_op jit(solution)/shard_map/all_gather | solution.py:22
  36.6 473.3 %all-gather.23.cloned.1.call-start = ((), (), s32[]{:S(2)}) async-start(), calls=%async_computation.7 | async-start | bytes 2506752 | tf_op jit(solution)/shard_map/all_gather | solution.py:62
  317.0 3.8 copy-start.2
  464.4 0.9 copy-start.3
  465.2 2.1 copy-start.5
  467.1 1.1 copy-start.4
  470.1 1.6 copy-start.8
  471.6 105.6 %all-gather.21.cloned.1.call-start = ((), (), s32[]{:S(2)}) async-start(), calls=%async_computation.6 | async-start | bytes 1114112 | tf_op jit(solution)/shard_map/all_gather | solution.py:34
  492.9 164.9 %all-gather.25.cloned.1.call-start = ((), (), s32[]{:S(2)}) async-start(), calls=%async_computation.8 | async-start | bytes 4734976 | tf_op jit(solution)/shard_map/all_gather | solution.py:62
  691.4 10.7 %copy-start.6 = (f32[1,2,512]{2,1,0:T(2,128)S(1)}, f32[1,2,512]{2,1,0:T(2,128)}, u32[]{:S(2)}) copy-start(f32[1,2,512]{2,1,0:T(2,128)} %get-tuple-element.67) | copy-start | bytes 12292
  692.2 9.8 %copy-start.7 = (f32[1,2,512]{2,1,0:T(2,128)S(1)}, f32[1,2,512]{2,1,0:T(2,128)}, u32[]{:S(2)}) copy-start(f32[1,2,512]{2,1,0:T(2,128)} %get-tuple-element.76) | copy-start | bytes 12292
Sparse Core Ops, SparseCore 0:
  13.0 302.6 all-reduce.1
  471.8 38.0 all-gather.22
  511.9 65.2 all-gather.20
  579.2 78.5 all-gather.24
Sparse Core Ops, SparseCore 1:
  33.7 106.3 all-gather.18
  143.5 142.1 all-gather.16
  288.5 145.9 all-gather.14
where the time goes:
time: 732 us; the launch traced here: 730 us
  waiting for transfers between devices  540 us (74%)
  blocking collectives  72.5 us (10%)
  local copies, waits for them, and re-layouts  65.7 us (9%)
  matrix products  18.4 us (3%)
  other arithmetic  17 us (2%)
  between operations  16.3 us (2%)
    psum x1, waiting for transfers between devices, per_device(): lax.psum(jnp.dot(onehot, embed, preferred_element_type=jnp.float32), WIDE)  277 us
    all_gather x2, waiting for transfers between devices, in_one_piece(): lax.all_gather(both, axis, axis=dim, tiled=True)  111 us
    all_gather x2, waiting for transfers between devices, collected_together(): both, at, found = (lax.all_gather(jnp.concatenate(lines), axis), 0, {})  95.9 us
    all_gather x2, waiting for transfers between devices, all_blocks(): tiles = lax.all_gather(tiles, axes[k])  54.6 us
    all_gather x2, blocking collectives, all_blocks(): tiles = lax.all_gather(tiles, axes[k])  44.4 us
    unnamed x47, local copies, waits for them, and re-layouts  27.5 us
    squeeze x74, local copies, waits for them, and re-layouts, joined_all(): x = combine(x, jax.tree.map(lambda part: part[k], pieces))  18.4 us
    all_to_all x1, blocking collectives, from_everyone(): return lax.all_to_all(copies, axis, split_axis=0, concat_axis=0, tiled=True)  15.5 us
  transfers between devices with their start and end apart: 7, of which 5 were waited for; matrix products, arithmetic and copies ran while one was open for 4% of the time, Pallas kernels for 0%

commit v1 on v0

--- a/solution.py
+++ b/solution.py
@@ -4,6 +4,7 @@
 from jax import lax
 from jax.sharding import Mesh
 from jax.sharding import PartitionSpec as P
+from jax.lax import psum
 
 HEAD_DIM = 64
 QUEST = 4
@@ -11,6 +12,11 @@
 GROUPS_WIDE = ("groups", "wide_0", "wide_1")
 EPS = 1e-06
 FLOOR = -1e30
+
+
+def note_clusters_by_axis(my_tile):
+    f_next = psum(psum(my_tile, "wide_1"), "wide_0")
+    return f_next
 
 
 def in_one_piece(arrays, axis, dim, along):
@@ -145,7 +151,7 @@
     onehot = (local_ids[:, None] == jnp.arange(vocab_rows, dtype=jnp.int32)[None, :]).astype(
         jnp.bfloat16
     )
-    embedded = lax.psum(jnp.dot(onehot, embed, preferred_element_type=jnp.float32), WIDE)
+    embedded = note_clusters_by_axis(jnp.dot(onehot, embed, preferred_element_type=jnp.float32))
     dec_in = rms_scale(embedded, dec_gain).astype(jnp.bfloat16)
     own_rows = lax.dynamic_slice_in_dim(dec_in, question * answers, answers, 0)
     proj_cols = key_w.shape[1]

time: 732 us -> 932 us (1.27)
  waiting for transfers between devices: 540 us -> 745 us
    all_gather x2, waiting for transfers between devices: 111 us -> 288 us  [in_one_piece(): lax.all_gather(both, axis, axis=dim, tiled=True)]
    all_gather x2, waiting for transfers between devices: 54.6 us -> 127 us  [all_blocks(): tiles = lax.all_gather(tiles, axes[k])]
    psum x1 -> x2, waiting for transfers between devices: 277 us -> 233 us  [note_clusters_by_axis(): f_next = psum(psum(my_tile, 'wide_1'), 'wide_0')]
    unnamed x47 -> x61, local copies, waits for them, and re-layouts: 27.5 us -> 27.4 us
  transfers between devices with their start and end apart: 7 -> 8, of which waited for: 5 -> 8; matrix products, arithmetic and copies ran while one was open for 4% -> 2% of each run, Pallas kernels for 0% -> 0%
where the time goes in v1:
time: 932 us; the launch traced here: 931 us
  waiting for transfers between devices  745 us (80%)
  blocking collectives  71.8 us (8%)
  local copies, waits for them, and re-layouts  65.5 us (7%)
  matrix products  18.4 us (2%)
  between operations  15.1 us (2%)
  other arithmetic  14.3 us (2%)
    all_gather x2, waiting for transfers between devices, in_one_piece(): lax.all_gather(both, axis, axis=dim, tiled=True)  288 us
    psum x2, waiting for transfers between devices, note_clusters_by_axis(): f_next = psum(psum(my_tile, 'wide_1'), 'wide_0')  233 us
    all_gather x2, waiting for transfers between devices, all_blocks(): tiles = lax.all_gather(tiles, axes[k])  127 us
    all_gather x2, waiting for transfers between devices, collected_together(): both, at, found = (lax.all_gather(jnp.concatenate(lines), axis), 0, {})  95.5 us
    all_gather x2, blocking collectives, all_blocks(): tiles = lax.all_gather(tiles, axes[k])  43.4 us
    unnamed x61, local copies, waits for them, and re-layouts  27.4 us
  transfers between devices with their start and end apart: 8, of which 8 were waited for; matrix products, arithmetic and copies ran while one was open for 2% of the time, Pallas kernels for 0%

profile of v1, /device:TPU:65, one launch (start us, length us, event | category | flops | bytes accessed | tf_op | source)
XLA Modules:
  0.0 930.7 jit_solution(16681242639916269181)
XLA Ops:
  7.4 0.9 broadcast_subtract_fusion
  8.3 1.1 fusion.40
  9.5 167.9 %all-reduce.3.cloned.1.call-done = f32[128,1024]{1,0:T(8,128)} async-done(((f32[128,1024]{1,0:T(8,128)}), f32[128,1024]{1,0:T(8,128)}) %all-reduce.3.cloned.1.call-update) | async-done | bytes 524304 | tf_op jit(solution)/shard_map/psum | solution.py:18
  177.6 22.1 %all-gather = bf16[11264,8]{0,1:T(8,128)(2,1)} all-gather(bf16[1408,8]{0,1:T(8,128)(2,1)} %param.18), channel_id=2, replica_groups=mesh['groups'=2,'wide_0'=8,'wide_1'=16,'narrow'=2] {'wide_0'}, dimensions={0}, use_global_device_ids=true | all-gather | bytes 202752 | tf_op jit(solution)/shard_map/all_gather | solution.py:40
  201.9 65.2 %all-reduce.5.cloned.1.call-done = f32[128,1024]{1,0:T(8,128)} async-done(((f32[128,1024]{1,0:T(8,128)}), f32[128,1024]{1,0:T(8,128)}) %all-reduce.5.cloned.1.call-update) | async-done | bytes 524304 | tf_op jit(solution)/shard_map/psum | solution.py:18
  267.1 1.2 multiply_reduce_fusion.1
  268.4 72.7 %all-gather.19.cloned.1.call-done = bf16[128,1408,8]{1,2,0:T(8,128)(2,1)} async-done(((bf16[8,1408,8]{1,2,0:T(8,128)(2,1)}), bf16[128,1408,8]{1,2,0:T(8,128)(2,1)}) %all-gather.19.cloned.1.call-update) | async-done | bytes 2883600 | tf_op jit(solution)/shard_map/all_gather | solution.py:40
  341.1 3.7 copy.413
  344.8 141.4 %all-gather.17.cloned.1.call-done = bf16[1024,1536]{1,0:T(8,128)(2,1)} async-done(((bf16[8,1536]{1,0:T(8,128)(2,1)}), bf16[1024,1536]{1,0:T(8,128)(2,1)}) %all-gather.17.cloned.1.call-update) | async-done | bytes 3145744 | tf_op jit(solution)/shard_map/all_gather | solution.py:28
  486.2 1.5 convolution_convert_fusion.3
  487.7 0.7 reshape.508
  488.5 147.0 %all-gather.15.cloned.1.call-done = bf16[1024,2816]{1,0:T(8,128)(2,1)} async-done(((bf16[8,2816]{1,0:T(8,128)(2,1)}), bf16[1024,2816]{1,0:T(8,128)(2,1)}) %all-gather.15.cloned.1.call-update) | async-done | bytes 5767184 | tf_op jit(solution)/shard_map/all_gather | solution.py:28
  635.5 4.9 fusion.12
  640.4 6.1 fusion.24
  647.0 15.8 %all_to_all.10 = f32[2,400,1024]{2,1,0:T(8,128)} all-to-all(f32[2,400,1024]{2,1,0:T(8,128)S(1)} %broadcast_in_dim.170), channel_id=1, replica_groups=mesh['groups'=2,'wide_0'=8,'wide_1'=16,'narrow'=2] {'narrow'}, dimensions={0} | all-to-all | bytes 6553600 | tf_op jit(solution)/shard_map/all_to_all | solution.py:53
  662.8 2.4 reduce_sum.55
  665.8 0.9 copy-done.3
  666.6 1.8 convolution_convert_fusion
  669.7 1.8 convolution_convert_fusion.1
  672.2 0.7 maximum_bitcast_fusion.1
  673.1 21.2 %all-gather.4 = bf16[4096,8]{0,1:T(8,128)(2,1)} all-gather(bf16[512,8]{0,1:T(8,128)(2,1)S(1)} %copy-done.10), channel_id=6, replica_groups=mesh['groups'=2,'wide_0'=8,'wide_1'=16,'narrow'=2] {'wide_0'}, dimensions={0}, use_global_device_ids=true | all-gather | bytes 73728 | tf_op jit(solution)/shard_map/all_gather | solution.py:40
  694.7 16.1 %all-gather.23.cloned.1.call-done = f32[8,132,512]{2,1,0:T(8,128)} async-done(((f32[1,132,512]{2,1,0:T(8,128)}), f32[8,132,512]{2,1,0:T(8,128)}) %all-gather.23.cloned.1.call-update) | async-done | bytes 2162704 | tf_op jit(solution)/shard_map/all_gather | solution.py:68
  710.8 1.0 fusion.51
  712.1 2.6 fusion.96
  715.3 1.1 copy.515
  716.4 1.8 copy.514
  718.2 0.8 copy.513
  719.0 0.8 fusion.95
  721.3 1.2 fusion.27
  722.7 0.9 copy.446
  723.6 54.7 %all-gather.21.cloned.1.call-done = bf16[128,512,8]{1,2,0:T(8,128)(2,1)} async-done(((bf16[8,512,8]{1,2,0:T(8,128)(2,1)}), bf16[128,512,8]{1,2,0:T(8,128)(2,1)}) %all-gather.21.cloned.1.call-update) | async-done | bytes 1048592 | tf_op jit(solution)/shard_map/all_gather | solution.py:40
  778.3 1.3 copy.511
  779.6 79.4 %all-gather.25.cloned.1.call-done = f32[16,132,512]{2,1,0:T(8,128)} async-done(((f32[1,132,512]{2,1,0:T(8,128)}), f32[16,132,512]{2,1,0:T(8,128)}) %all-gather.25.cloned.1.call-update) | async-done | bytes 4325392 | tf_op jit(solution)/shard_map/all_gather | solution.py:68
  859.0 3.8 fusion.94
  863.4 1.1 copy.532
  864.5 1.8 copy.531
  866.3 1.8 copy.530
  868.0 1.8 copy.529
  869.8 1.8 copy.528
  871.6 1.8 copy.527
  873.4 1.8 copy.526
  875.2 1.8 copy.525
  877.0 1.8 copy.524
  878.8 1.8 copy.523
  880.6 1.8 copy.522
  882.4 1.8 copy.521
  884.1 1.5 fusion.93
  886.6 1.6 fusion.92
  888.2 0.8 squeeze.305
  889.6 0.8 squeeze.304
  891.1 0.8 squeeze.303
  893.4 0.7 copy.500
  894.9 0.7 copy.498
  897.8 0.8 squeeze.265
  899.8 0.8 squeeze.276
  900.6 0.8 squeeze.274
  901.4 0.8 squeeze.272
  902.3 0.8 squeeze.270
  903.5 0.8 squeeze.292
  904.9 0.8 squeeze.294
  906.4 1.0 multiply_add_fusion
  907.3 2.6 divide_convert_fusion
  910.4 12.7 %all_to_all.11 = bf16[2,128,512]{2,1,0:T(8,128)(2,1)S(1)} all-to-all(bf16[2,128,512]{2,1,0:T(8,128)(2,1)S(1)} %bitcast.360), channel_id=1, replica_groups=mesh['groups'=2,'wide_0'=8,'wide_1'=16,'narrow'=2] {'narrow'}, dimensions={0} | all-to-all | bytes 524288 | tf_op jit(solution)/shard_map/all_to_all | solution.py:94
  923.1 0.7 add_convert_fusion
  (171 shorter events, 19.0 us)
Async XLA Ops:
  7.2 1.2 copy-start
  7.2 192.7 %copy-start.11 = (bf16[8,512]{1,0:T(8,128)(2,1)S(1)}, bf16[8,512]{1,0:T(8,128)(2,1)}, u32[]{:S(2)}) copy-start(bf16[8,512]{1,0:T(8,128)(2,1)} %param.22) | copy-start | bytes 24580
  7.2 192.7 %copy-start.12 = (bf16[8,512]{1,0:T(8,128)(2,1)S(1)}, bf16[8,512]{1,0:T(8,128)(2,1)}, u32[]{:S(2)}) copy-start(bf16[8,512]{1,0:T(8,128)(2,1)} %param.21) | copy-start | bytes 24580
  7.2 192.7 %copy-start.13 = (bf16[8,512]{1,0:T(8,128)(2,1)S(1)}, bf16[8,512]{1,0:T(8,128)(2,1)}, u32[]{:S(2)}) copy-start(bf16[8,512]{1,0:T(8,128)(2,1)} %param.20) | copy-start | bytes 24580
  7.2 193.4 %copy-start.6 = (bf16[8,1408]{1,0:T(8,128)(2,1)S(1)}, bf16[8,1408]{1,0:T(8,128)(2,1)}, u32[]{:S(2)}) copy-start(bf16[8,1408]{1,0:T(8,128)(2,1)} %param.17) | copy-start | bytes 67588
  7.2 193.4 %copy-start.7 = (bf16[8,1408]{1,0:T(8,128)(2,1)S(1)}, bf16[8,1408]{1,0:T(8,128)(2,1)}, u32[]{:S(2)}) copy-start(bf16[8,1408]{1,0:T(8,128)(2,1)} %param.16) | copy-start | bytes 67588
  7.2 194.2 %copy-start.14 = (bf16[1024]{0:T(1024)(128)(2,1)S(1)}, bf16[1024]{0:T(1024)(128)(2,1)}, u32[]{:S(2)}) copy-start(bf16[1024]{0:T(1024)(128)(2,1)} %param.15) | copy-start | bytes 6148
  7.3 194.2 %copy-start.15 = (bf16[1024]{0:T(1024)(128)(2,1)S(1)}, bf16[1024]{0:T(1024)(128)(2,1)}, u32[]{:S(2)}) copy-start(bf16[1024]{0:T(1024)(128)(2,1)} %param.19) | copy-start | bytes 6148
  7.3 194.2 %copy-start.16 = (bf16[1024]{0:T(1024)(128)(2,1)S(1)}, bf16[1024]{0:T(1024)(128)(2,1)}, u32[]{:S(2)}) copy-start(bf16[1024]{0:T(1024)(128)(2,1)} %param.24) | copy-start | bytes 6148
  7.3 194.2 %copy-start.17 = (s32[2]{0:T(128)S(1)}, s32[2]{0:T(128)}, u32[]{:S(2)}) copy-start(s32[2]{0:T(128)} %param.26) | copy-start | bytes 28
  7.3 194.4 %copy-start.1 = (bf16[400,1024]{1,0:T(8,128)(2,1)S(1)}, bf16[400,1024]{1,0:T(8,128)(2,1)}, u32[]{:S(2)}) copy-start(bf16[400,1024]{1,0:T(8,128)(2,1)} %param.14) | copy-start | bytes 2457604
  7.3 170.1 %all-reduce.3.cloned.1.call-start = ((), (), s32[]{:S(2)}) async-start(), calls=%async_computation.3 | async-start | bytes 1048576 | tf_op jit(solution)/shard_map/psum | solution.py:18
  9.5 257.7 %all-reduce.5.cloned.1.call-start = ((), (), s32[]{:S(2)}) async-start(), calls=%async_computation.4 | async-start | bytes 1048576 | tf_op jit(solution)/shard_map/psum | solution.py:18
  177.5 163.6 %all-gather.19.cloned.1.call-start = ((), (), s32[]{:S(2)}) async-start(), calls=%async_computation.6 | async-start | bytes 3063808 | tf_op jit(solution)/shard_map/all_gather | solution.py:40
  199.8 286.4 %all-gather.17.cloned.1.call-start = ((), (), s32[]{:S(2)}) async-start(), calls=%async_computation.5 | async-start | bytes 3170304 | tf_op jit(solution)/shard_map/all_gather | solution.py:28
  200.6 434.9 %all-gather.15.cloned.1.call-start = ((), (), s32[]{:S(2)}) async-start(), calls=%async_computation.2 | async-start | bytes 5812224 | tf_op jit(solution)/shard_map/all_gather | solution.py:28
  201.3 509.5 %all-gather.23.cloned.1.call-start = ((), (), s32[]{:S(2)}) async-start(), calls=%async_computation.8 | async-start | bytes 2506752 | tf_op jit(solution)/shard_map/all_gather | solution.py:68
  341.1 145.1 %copy-start.2 = (f32[128,1024]{1,0:T(8,128)S(1)}, f32[128,1024]{1,0:T(8,128)}, u32[]{:S(2)}) copy-start(f32[128,1024]{1,0:T(8,128)} %all-reduce.5.cloned.1.call-done) | copy-start | bytes 1572868
  665.7 0.9 copy-start.3
  666.6 2.1 copy-start.5
  668.5 1.1 copy-start.4
  671.5 1.6 copy-start.10
  673.0 105.3 %all-gather.21.cloned.1.call-start = ((), (), s32[]{:S(2)}) async-start(), calls=%async_computation.7 | async-start | bytes 1114112 | tf_op jit(solution)/shard_map/all_gather | solution.py:40
  694.4 164.6 %all-gather.25.cloned.1.call-start = ((), (), s32[]{:S(2)}) async-start(), calls=%async_computation.9 | async-start | bytes 4734976 | tf_op jit(solution)/shard_map/all_gather | solution.py:68
  892.6 10.7 %copy-start.8 = (f32[1,2,512]{2,1,0:T(2,128)S(1)}, f32[1,2,512]{2,1,0:T(2,128)}, u32[]{:S(2)}) copy-start(f32[1,2,512]{2,1,0:T(2,128)} %get-tuple-element.67) | copy-start | bytes 12292
  893.3 9.8 %copy-start.9 = (f32[1,2,512]{2,1,0:T(2,128)S(1)}, f32[1,2,512]{2,1,0:T(2,128)}, u32[]{:S(2)}) copy-start(f32[1,2,512]{2,1,0:T(2,128)} %get-tuple-element.76) | copy-start | bytes 12292
Sparse Core Ops, SparseCore 0:
  11.0 166.3 all-reduce.2
  179.8 87.3 all-reduce.4
  269.3 71.7 all-gather.18
  344.5 141.6 all-gather.16
  489.6 145.8 all-gather.14
  673.2 37.5 all-gather.22
  712.9 65.3 all-gather.20
  780.4 78.5 all-gather.24
